TPU v7x, 32 devices: a whole 2x2x4 slice. The times are simulated.
32 devices in a mesh: groups: 2 (over y), rows: 4 (over z), keys: 2 (over x), heads: 2 (over core).
Axes of the slice: x: 2, y: 2, z: 4, core: 2. Of those that a mesh axis runs over, the one named last changes fastest.
Arguments:
- pair: bfloat16 [1024, 512, 128], P(('groups', 'rows'), 'keys'), parts along dimension 0, may hold values from -6 to 6
- seq_length: int32 [2], P('groups'), parts along dimension 0, may hold values from 257 to 512
- tile_counts: int32 [1024, 4], P(('groups', 'rows')), parts along dimension 0, may hold values from 0 to 128, as said below
- ln_gain: float32 [128], replicated, may hold values from 0.5 to 1.5
- w_query: bfloat16 [128, 128], P(None, 'heads'), may hold values from -8 to 8
- w_key: bfloat16 [128, 128], P(None, 'heads'), may hold values from -0.5 to 0.5
- w_value: bfloat16 [128, 128], P(None, 'heads'), may hold values from -0.5 to 0.5
- w_gate: bfloat16 [128, 128], P(None, 'heads'), may hold values from -0.5 to 0.5
- w_bias: bfloat16 [128, 4], P(None, 'heads'), may hold values from -1.5 to 1.5
- w_out: bfloat16 [128, 128], replicated, may hold values from -2 to 2
Outputs:
- update: bfloat16 [1024, 512, 128], P(('groups', 'rows'), ('keys', 'heads')), parts along dimension 0
There are 2 independent parts, one for each index of `groups`. A program takes and returns all parts, laid end to end along the dimension named above; an argument that names none is the same for every part. Nothing has to cross between parts.
Inputs may be any that keep to these rules, and one draw needn't show every extreme that they name: `tile_counts`: for each row and each tile of 128 keys, how many of the tile's leading keys are valid; some rows have no valid key at all.
All inputs are finite; a program needn't handle non-finite values.
Results may differ from a plain program's by a relative error of at most 0.03.
The roundings to bfloat16 on the way count: a program that leaves them out, or rounds other values in their place, can miss the bound.
Values may be sent and summed in bfloat16 or wider, within the bound.
A program may use at most 192 MiB of HBM per device.

v0:
```python
import jax
import jax.numpy as jnp
from jax import lax
from jax.sharding import PartitionSpec as P

HEAD_DIM = 32
TILE = 128
norm_epsilon = 1e-05
masked_score = -1e30


def layer_norm(values, gain):
    center = values - jnp.mean(values, axis=-1, keepdims=True)
    spread = jnp.mean(center * center, axis=-1, keepdims=True)
    return center * lax.rsqrt(spread + norm_epsilon) * gain


def finish(row_sum, weighted):
    denom = jnp.maximum(row_sum, 1.0)
    result = weighted / denom[..., None]
    rows_dev, heads_dev, cols_dev, depth = result.shape
    result = jnp.transpose(result, (0, 2, 1, 3)).reshape(rows_dev, cols_dev, heads_dev * depth)
    return result.astype(jnp.bfloat16)


def per_device(
    pair, seq_length, tile_counts, ln_gain, w_query, w_key, w_value, w_gate, w_bias, w_out
):
    rows_dev, cols_dev, channels = pair.shape
    key_groups = lax.axis_size("keys")
    length_all = cols_dev * key_groups
    heads_dev = w_bias.shape[1]
    width_dev = heads_dev * HEAD_DIM
    normed = layer_norm(pair.astype(jnp.float32), ln_gain).astype(jnp.bfloat16)
    flat = normed.reshape(rows_dev * cols_dev, channels)
    queries = (
        (jnp.dot(flat, w_query, preferred_element_type=jnp.float32) * HEAD_DIM ** (-0.5))
        .astype(jnp.bfloat16)
        .reshape(rows_dev, cols_dev, heads_dev, HEAD_DIM)
    )
    keys_local = (
        jnp.dot(flat, w_key, preferred_element_type=jnp.float32)
        .astype(jnp.bfloat16)
        .reshape(rows_dev, cols_dev, heads_dev, HEAD_DIM)
    )
    values_local = (
        jnp.dot(flat, w_value, preferred_element_type=jnp.float32)
        .astype(jnp.bfloat16)
        .reshape(rows_dev, cols_dev, heads_dev, HEAD_DIM)
    )
    gate_act = jax.nn.sigmoid(jnp.dot(flat, w_gate, preferred_element_type=jnp.float32)).reshape(
        rows_dev, cols_dev, width_dev
    )
    bias_local = jnp.einsum("rkc,ch->hrk", normed, w_bias, preferred_element_type=jnp.float32)
    bias_rows = lax.all_gather(bias_local.astype(jnp.bfloat16), "rows", axis=1, tiled=True).astype(
        bias_local.dtype
    )
    positions = jnp.arange(length_all, dtype=jnp.int32)
    allowed = (positions[None, :] < seq_length[0]) & (
        (positions % TILE)[None, :] < jnp.repeat(tile_counts, TILE, axis=1)
    )
    bias_turn = lax.all_to_all(
        bias_rows.astype(jnp.bfloat16), "keys", split_axis=1, concat_axis=2, tiled=True
    ).astype(bias_rows.dtype)
    initial = (
        jnp.full((rows_dev, heads_dev, cols_dev), masked_score, jnp.float32),
        jnp.zeros((rows_dev, heads_dev, cols_dev), jnp.float32),
        jnp.zeros((rows_dev, heads_dev, cols_dev, HEAD_DIM), jnp.float32),
    )
    piece_keys = lax.all_gather(keys_local, "keys", axis=1, tiled=True)
    piece_values = lax.all_gather(values_local, "keys", axis=1, tiled=True)

    def one_tile(tile_index, state):
        row_max, row_sum, weighted = state
        offset = tile_index * TILE
        key_tile = lax.dynamic_slice_in_dim(piece_keys, offset, TILE, 1)
        value_tile = lax.dynamic_slice_in_dim(piece_values, offset, TILE, 1)
        tile_bias = lax.dynamic_slice_in_dim(bias_turn, offset, TILE, 2)
        shown = lax.dynamic_slice_in_dim(allowed, offset, TILE, 1)[:, None, None, :]
        scores = (
            jnp.einsum("rjhd,rkhd->rhjk", queries, key_tile, preferred_element_type=jnp.float32)
            + tile_bias[None]
        )
        scores = jnp.where(shown, scores, masked_score)
        new_max = jnp.maximum(row_max, jnp.max(scores, axis=-1))
        weights = jnp.where(shown, jnp.exp(scores - new_max[..., None]), 0.0)
        rescale = jnp.exp(row_max - new_max)
        row_sum = row_sum * rescale + jnp.sum(weights, axis=-1)
        weighted = weighted * rescale[..., None] + jnp.einsum(
            "rhjk,rkhd->rhjd",
            weights.astype(jnp.bfloat16),
            value_tile,
            preferred_element_type=jnp.float32,
        )
        return (new_max, row_sum, weighted)

    row_max, row_sum, weighted = lax.fori_loop(0, piece_keys.shape[1] // TILE, one_tile, initial)
    attended = finish(row_sum, weighted)
    attended = lax.optimization_barrier(attended).astype(jnp.float32)
    gated = (gate_act * attended).astype(jnp.bfloat16)
    head_rank = lax.axis_index("heads")
    w_rows = lax.dynamic_slice_in_dim(w_out, head_rank * width_dev, width_dev, 0)
    partial_out = jnp.einsum("rkc,cd->rkd", gated, w_rows, preferred_element_type=jnp.float32)
    return lax.psum_scatter(
        partial_out.astype(jnp.bfloat16), "heads", scatter_dimension=1, tiled=True
    )


def solution(mesh):
    in_specs = (
        P(("groups", "rows"), "keys", None),
        P("groups"),
        P(("groups", "rows"), None),
        P(),
        P(None, "heads"),
        P(None, "heads"),
        P(None, "heads"),
        P(None, "heads"),
        P(None, "heads"),
        P(),
    )
    out_specs = P(("groups", "rows"), ("keys", "heads"), None)
    return jax.shard_map(
        per_device, mesh=mesh, in_specs=in_specs, out_specs=out_specs, check_vma=False
    )
```

profile of v0, /device:TPU:0, one launch (start us, length us, event | category | flops | bytes accessed | tf_op | source)
XLA Modules:
  0.0 505.1 jit_solution(12324241964965826432)
XLA Ops:
  6.5 5.8 %convert_reduce_fusion = f32[128,256]{1,0:T(8,128)S(1)} fusion(bf16[128,256,128]{2,1,0:T(8,128)(2,1)} %param.12), kind=kLoop, calls=%fused_computation.33 | loop fusion | flops 8355840 | bytes 8519680 | tf_op jit(solution)/shard_map/reduce_sum | solution.py:13
  12.4 0.0 slice-start.1
  12.4 10.9 %fusion.25 = f32[128,256]{1,0:T(8,128)S(1)} fusion(bf16[128,256,128]{2,1,0:T(8,128)(2,1)} %param.12, f32[128,256]{1,0:T(8,128)S(1)} %broadcast_multiply_fusion), kind=kLoop, calls=%fused_computation.36 | loop fusion | flops 16744448 | bytes 8650752 | tf_op jit(solution)/shard_map/reduce_sum | solution.py:14
  23.3 9.9 %fusion.27 = bf16[128,256,128]{2,1,0:T(8,128)(2,1)S(1)} fusion(bf16[128,256,128]{2,1,0:T(8,128)(2,1)S(1)} %bitcast.83, f32[128]{0:T(128)S(1)} %copy-done.9, f32[128,256]{1,0:T(8,128)S(1)} %add_rsqrt_fusion, f32[128,256]{1,0:T(8,128)S(1)} %broadcast_multiply_fusion), kind=kLoop, calls=%fused_computation.38 | loop fusion | flops 20971520 | bytes 17039872 | tf_op jit(solution)/shard_map/convert_element_type | solution.py:34
  33.3 3.2 copy-done.1
  36.5 3.0 convolution_convert_fusion.1
  39.5 1.1 copy.28
  40.6 0.0 copy-start.6
  40.6 4.4 copy.20
  45.1 0.0 all-gather.3.cloned.1.call-update
  45.1 0.2 all-gather.5.cloned.1.call-start
  45.3 6.4 %convolution_convert_fusion = bf16[32768,64]{0,1:T(8,128)(2,1)S(1)} fusion(bf16[32768,128]{1,0:T(8,128)(2,1)} %bitcast.79, bf16[128,64]{0,1:T(8,128)(2,1)S(1)} %copy-done.6), kind=kOutput, calls=%fused_computation.29 | convolution fusion | flops 538968064 | bytes 12599296 | tf_op jit(solution)/shard_map/dot_general | solution.py:47
  51.7 1.1 copy.30
  52.8 0.0 copy-start.10
  52.9 4.6 copy.22
  57.5 0.0 all-gather.5.cloned.1.call-update
  57.5 0.0 copy-start.7
  57.5 6.8 %fusion.30 = bf16[2,128,256]{2,0,1:T(2,128)(2,1)S(1)} fusion(bf16[128,256,128]{2,1,0:T(8,128)(2,1)} %copy-done.1, bf16[128,2]{0,1:T(2,128)(2,1)S(1)} %copy-done.10), kind=kOutput, calls=%fused_computation.44 | convolution fusion | flops 16842752 | bytes 8520192 | tf_op jit(solution)/shard_map/rkc,ch->hrk/dot_general | solution.py:54
  64.3 17.8 %all_gather.10 = bf16[2,512,256]{2,0,1:T(2,128)(2,1)} all-gather(bf16[2,128,256]{2,0,1:T(2,128)(2,1)S(1)} %fusion.30), channel_id=1, replica_groups=mesh['groups'=2,'rows'=4,'keys'=2,'heads'=2] {'rows'}, dimensions={1}, use_global_device_ids=true | all-gather | bytes 655360 | tf_op jit(solution)/shard_map/all_gather | solution.py:55
  82.1 3.5 all-to-all-start
  85.6 0.3 reduce-scatter.2.cloned.1.call-start
  86.5 8.3 %fusion.21 = bf16[32768,64]{0,1:T(8,128)(2,1)} fusion(bf16[32768,128]{1,0:T(8,128)(2,1)} %bitcast.80, bf16[128,64]{0,1:T(8,128)(2,1)S(1)} %copy-done.7), kind=kOutput, calls=%fused_computation.28 | convolution fusion | flops 541065216 | bytes 12599296 | tf_op jit(solution)/shard_map/dot_general | solution.py:37
  94.9 9.7 %fusion.22 = f32[32768,64]{0,1:T(8,128)} fusion(bf16[32768,128]{1,0:T(8,128)(2,1)} %bitcast.81, bf16[128,64]{0,1:T(8,128)(2,1)S(1)} %copy-done.11), kind=kOutput, calls=%fused_computation.31 | convolution fusion | flops 543162368 | bytes 16793600 | tf_op jit(solution)/shard_map/dot_general | solution.py:51
  104.5 0.0 copy-start.8
  104.6 3.3 copy.29
  107.8 4.4 copy.23
  112.3 0.1 copy.19
  112.4 0.2 broadcast_in_dim.67
  112.6 0.1 fusion.31
  112.6 0.4 convert_bitcast_fusion
  113.0 0.8 copy.21
  113.8 43.7 %all-gather.3.cloned.1.call-done = bf16[128,512,2,32]{1,3,2,0:T(8,128)(2,1)} async-done(((bf16[128,256,2,32]{1,3,2,0:T(8,128)(2,1)}), bf16[128,512,2,32]{1,3,2,0:T(8,128)(2,1)}) %all-gather.3.cloned.1.call-update) | async-done | bytes 8388624 | tf_op jit(solution)/shard_map/all_gather | solution.py:70
  157.5 105.5 %all-gather.5.cloned.1.call-done = bf16[128,512,2,32]{1,3,2,0:T(8,128)(2,1)} async-done(((bf16[128,256,2,32]{1,3,2,0:T(8,128)(2,1)}), bf16[128,512,2,32]{1,3,2,0:T(8,128)(2,1)}) %all-gather.5.cloned.1.call-update) | async-done | bytes 8388624 | tf_op jit(solution)/shard_map/all_gather | solution.py:71
  263.1 208.6 %while.18 = (s32[]{:T(128)}, f32[128,2,256]{2,1,0:T(2,128)S(1)}, f32[128,2,256]{2,1,0:T(2,128)S(1)}, f32[128,2,256,32]{2,3,1,0:T(8,128)}, pred[128,512]{1,0:T(8,...) while((s32[]{:T(128)}, f32[128,2,256]{2,1,0:T(2,128)S(1)}, ...), condition=%wide.region_5.6_spmd.clone, body=%wide.region_2.5_spmd.clone.sunk | while | flops 1189412864 | bytes 198525168 | solution.py:97
  263.1 16.2 %fusion.60 = (f32[128,2,256]{2,1,0:T(2,128)S(1)}, f32[128,2,128,256]{3,2,1,0:T(8,128)}) fusion(f32[2,256,128]{1,2,0:T(8,128)S(1)} %constant_dynamic-slice_fusion.4, pred[128,128]{1,0:T(8,128)(4,1)S(1)} %constant_dynamic-slice_fusion.5, bf16[128,256,2,32]{1,3,2,0:T(8,128)(2,1)} %get-tuple-element.327, ...), kind=kOutput, calls=%fused_computation.3.clone.1 | convolution fusion | flops 561971200 | bytes 40386564 | tf_op jit(solution)/shard_map/while/body/eval_jaxpr/rjhd,rkhd->rhjk/dot_general | solution.py:81
  279.3 0.2 fusion.61
  279.5 16.8 %fusion.62 = f32[128,2,256]{2,1,0:T(2,128)S(1)} fusion(f32[128,2,128,256]{3,2,1,0:T(8,128)} %get-tuple-element.292, f32[128,2,256]{2,1,0:T(2,128)S(1)} %fusion.61, f32[2,256,128]{1,2,0:T(8,128)S(1)} %constant_dynamic-slice_fusion.4, pred[128,128]{1,0:T(8,128)(4,1)S(1)} %constant_dynamic-slice_fusion.5), kind=kLoop, calls=%fused_computation.5.clone.1 | loop fusion | flops 41877504 | bytes 34357248 | tf_op jit(solution)/shard_map/while/body/eval_jaxpr/reduce_sum | solution.py:88
  296.3 0.6 fusion.63
  296.9 15.0 %fusion.64 = f32[128,2,256,32]{2,3,1,0:T(8,128)S(1)} fusion(f32[128,2,256,32]{2,3,1,0:T(8,128)S(1)} %copy-done.2, f32[128,2,256]{2,1,0:T(2,128)S(1)} %get-tuple-element.294, pred[]{:T(512)S(6)} %compare.4, f32[128,2,128,256]{3,2,1,0:T(8,128)} %get-tuple-element.292, f32[128,2,256]{2,1,0:T(2,128)S(1)} %fusion.61, ...), kind=kOutput, calls=%fused_computation.9.clone.1 | convolution fusion | flops 585105408 | bytes 53231620 | tf_op jit(solution)/shard_map/while/body/eval_jaxpr/rhjk,rkhd->rhjd/dot_general | solution.py:89
  311.9 3.2 copy-done.3
  315.3 16.2 %fusion.60 = (f32[128,2,256]{2,1,0:T(2,128)S(1)}, f32[128,2,128,256]{3,2,1,0:T(8,128)}) fusion(f32[2,256,128]{1,2,0:T(8,128)S(1)} %constant_dynamic-slice_fusion.4, pred[128,128]{1,0:T(8,128)(4,1)S(1)} %constant_dynamic-slice_fusion.5, bf16[128,256,2,32]{1,3,2,0:T(8,128)(2,1)} %get-tuple-element.327, ...), kind=kOutput, calls=%fused_computation.3.clone.1 | convolution fusion | flops 561971200 | bytes 40386564 | tf_op jit(solution)/shard_map/while/body/eval_jaxpr/rjhd,rkhd->rhjk/dot_general | solution.py:81
  331.5 0.2 fusion.61
  331.7 16.8 %fusion.62 = f32[128,2,256]{2,1,0:T(2,128)S(1)} fusion(f32[128,2,128,256]{3,2,1,0:T(8,128)} %get-tuple-element.292, f32[128,2,256]{2,1,0:T(2,128)S(1)} %fusion.61, f32[2,256,128]{1,2,0:T(8,128)S(1)} %constant_dynamic-slice_fusion.4, pred[128,128]{1,0:T(8,128)(4,1)S(1)} %constant_dynamic-slice_fusion.5), kind=kLoop, calls=%fused_computation.5.clone.1 | loop fusion | flops 41877504 | bytes 34357248 | tf_op jit(solution)/shard_map/while/body/eval_jaxpr/reduce_sum | solution.py:88
  348.5 0.6 fusion.63
  349.0 15.0 %fusion.64 = f32[128,2,256,32]{2,3,1,0:T(8,128)S(1)} fusion(f32[128,2,256,32]{2,3,1,0:T(8,128)S(1)} %copy-done.2, f32[128,2,256]{2,1,0:T(2,128)S(1)} %get-tuple-element.294, pred[]{:T(512)S(6)} %compare.4, f32[128,2,128,256]{3,2,1,0:T(8,128)} %get-tuple-element.292, f32[128,2,256]{2,1,0:T(2,128)S(1)} %fusion.61, ...), kind=kOutput, calls=%fused_computation.9.clone.1 | convolution fusion | flops 585105408 | bytes 53231620 | tf_op jit(solution)/shard_map/while/body/eval_jaxpr/rhjk,rkhd->rhjd/dot_general | solution.py:89
  364.1 3.2 copy-done.3
  367.4 16.2 %fusion.60 = (f32[128,2,256]{2,1,0:T(2,128)S(1)}, f32[128,2,128,256]{3,2,1,0:T(8,128)}) fusion(f32[2,256,128]{1,2,0:T(8,128)S(1)} %constant_dynamic-slice_fusion.4, pred[128,128]{1,0:T(8,128)(4,1)S(1)} %constant_dynamic-slice_fusion.5, bf16[128,256,2,32]{1,3,2,0:T(8,128)(2,1)} %get-tuple-element.327, ...), kind=kOutput, calls=%fused_computation.3.clone.1 | convolution fusion | flops 561971200 | bytes 40386564 | tf_op jit(solution)/shard_map/while/body/eval_jaxpr/rjhd,rkhd->rhjk/dot_general | solution.py:81
  383.6 0.2 fusion.61
  383.8 16.8 %fusion.62 = f32[128,2,256]{2,1,0:T(2,128)S(1)} fusion(f32[128,2,128,256]{3,2,1,0:T(8,128)} %get-tuple-element.292, f32[128,2,256]{2,1,0:T(2,128)S(1)} %fusion.61, f32[2,256,128]{1,2,0:T(8,128)S(1)} %constant_dynamic-slice_fusion.4, pred[128,128]{1,0:T(8,128)(4,1)S(1)} %constant_dynamic-slice_fusion.5), kind=kLoop, calls=%fused_computation.5.clone.1 | loop fusion | flops 41877504 | bytes 34357248 | tf_op jit(solution)/shard_map/while/body/eval_jaxpr/reduce_sum | solution.py:88
  400.6 0.6 fusion.63
  401.2 15.0 %fusion.64 = f32[128,2,256,32]{2,3,1,0:T(8,128)S(1)} fusion(f32[128,2,256,32]{2,3,1,0:T(8,128)S(1)} %copy-done.2, f32[128,2,256]{2,1,0:T(2,128)S(1)} %get-tuple-element.294, pred[]{:T(512)S(6)} %compare.4, f32[128,2,128,256]{3,2,1,0:T(8,128)} %get-tuple-element.292, f32[128,2,256]{2,1,0:T(2,128)S(1)} %fusion.61, ...), kind=kOutput, calls=%fused_computation.9.clone.1 | convolution fusion | flops 585105408 | bytes 53231620 | tf_op jit(solution)/shard_map/while/body/eval_jaxpr/rhjk,rkhd->rhjd/dot_general | solution.py:89
  416.3 3.2 copy-done.3
  419.6 16.2 %fusion.60 = (f32[128,2,256]{2,1,0:T(2,128)S(1)}, f32[128,2,128,256]{3,2,1,0:T(8,128)}) fusion(f32[2,256,128]{1,2,0:T(8,128)S(1)} %constant_dynamic-slice_fusion.4, pred[128,128]{1,0:T(8,128)(4,1)S(1)} %constant_dynamic-slice_fusion.5, bf16[128,256,2,32]{1,3,2,0:T(8,128)(2,1)} %get-tuple-element.327, ...), kind=kOutput, calls=%fused_computation.3.clone.1 | convolution fusion | flops 561971200 | bytes 40386564 | tf_op jit(solution)/shard_map/while/body/eval_jaxpr/rjhd,rkhd->rhjk/dot_general | solution.py:81
  435.8 0.2 fusion.61
  436.0 16.8 %fusion.62 = f32[128,2,256]{2,1,0:T(2,128)S(1)} fusion(f32[128,2,128,256]{3,2,1,0:T(8,128)} %get-tuple-element.292, f32[128,2,256]{2,1,0:T(2,128)S(1)} %fusion.61, f32[2,256,128]{1,2,0:T(8,128)S(1)} %constant_dynamic-slice_fusion.4, pred[128,128]{1,0:T(8,128)(4,1)S(1)} %constant_dynamic-slice_fusion.5), kind=kLoop, calls=%fused_computation.5.clone.1 | loop fusion | flops 41877504 | bytes 34357248 | tf_op jit(solution)/shard_map/while/body/eval_jaxpr/reduce_sum | solution.py:88
  452.8 0.6 fusion.63
  453.4 15.0 %fusion.64 = f32[128,2,256,32]{2,3,1,0:T(8,128)S(1)} fusion(f32[128,2,256,32]{2,3,1,0:T(8,128)S(1)} %copy-done.2, f32[128,2,256]{2,1,0:T(2,128)S(1)} %get-tuple-element.294, pred[]{:T(512)S(6)} %compare.4, f32[128,2,128,256]{3,2,1,0:T(8,128)} %get-tuple-element.292, f32[128,2,256]{2,1,0:T(2,128)S(1)} %fusion.61, ...), kind=kOutput, calls=%fused_computation.9.clone.1 | convolution fusion | flops 585105408 | bytes 53231620 | tf_op jit(solution)/shard_map/while/body/eval_jaxpr/rhjk,rkhd->rhjd/dot_general | solution.py:89
  468.4 3.2 copy-done.3
  471.7 0.1 broadcast_maximum_fusion
  471.8 5.0 divide_convert_fusion
  476.8 0.7 copy-done.4
  477.6 4.6 convolution_convert_fusion.2
  482.2 0.0 reduce-scatter.2.cloned.1.call-update
  482.2 16.4 %reduce-scatter.2.cloned.1.call-done = bf16[128,128,128]{2,1,0:T(8,128)(2,1)} async-done(((bf16[128,256,128]{2,1,0:T(8,128)(2,1)}), bf16[128,128,128]{2,1,0:T(8,128)(2,1)}) %reduce-scatter.2.cloned.1.call-update) | async-done | bytes 4194320 | tf_op jit(solution)/shard_map/reduce_scatter | solution.py:104
  (51 shorter events, 0.3 us)
Async XLA Ops:
  6.5 470.3 %copy-start = (bf16[128,128]{1,0:T(8,128)(2,1)S(1)}, bf16[128,128]{1,0:T(8,128)(2,1)}, u32[]{:S(2)}) copy-start(bf16[128,128]{1,0:T(8,128)(2,1)} %param.21) | copy-start | bytes 98308
  6.5 16.8 %copy-start.9 = (f32[128]{0:T(128)S(1)}, f32[128]{0:T(128)}, u32[]{:S(2)}) copy-start(f32[128]{0:T(128)} %param.15) | copy-start | bytes 1540
  6.5 151.0 %all-gather.3.cloned.1.call-start = ((), (), s32[]{:S(2)}) async-start(), calls=%async_computation.2 | async-start | bytes 12582912 | tf_op jit(solution)/shard_map/all_gather | solution.py:70
  6.5 16.8 %slice-start = ((s8[8388608]{0:T(1024)(128)(4,1)}), s8[4194304]{0:T(1024)(128)(4,1)S(1)}, s32[]{:S(2)}) async-start(s8[8388608]{0:T(1024)(128)(4,1)} %bitcast.82), calls=%async_computation.5 | async-start | bytes 8388608
  12.4 10.9 %slice-start.1 = ((s8[8388608]{0:T(1024)(128)(4,1)}), s8[4194304]{0:T(1024)(128)(4,1)S(1)}, s32[]{:S(2)}) async-start(s8[8388608]{0:T(1024)(128)(4,1)} %bitcast.82), calls=%async_computation.6 | async-start | bytes 8388608
  23.3 13.2 %copy-start.5 = (bf16[128,64]{0,1:T(8,128)(2,1)S(1)}, bf16[128,64]{0,1:T(8,128)(2,1)}, u32[]{:S(2)}) copy-start(bf16[128,64]{0,1:T(8,128)(2,1)} %param.17) | copy-start | bytes 49156
  33.3 3.2 copy-start.1
  40.6 4.7 copy-start.6
  45.1 218.0 %all-gather.5.cloned.1.call-start = ((), (), s32[]{:S(2)}) async-start(), calls=%async_computation.3 | async-start | bytes 12582912 | tf_op jit(solution)/shard_map/all_gather | solution.py:71
  52.8 4.7 copy-start.10
  57.5 29.0 %copy-start.7 = (bf16[128,64]{0,1:T(8,128)(2,1)S(1)}, bf16[128,64]{0,1:T(8,128)(2,1)}, u32[]{:S(2)}) copy-start(bf16[128,64]{0,1:T(8,128)(2,1)} %param.16) | copy-start | bytes 49156
  64.3 30.6 %copy-start.11 = (bf16[128,64]{0,1:T(8,128)(2,1)S(1)}, bf16[128,64]{0,1:T(8,128)(2,1)}, u32[]{:S(2)}) copy-start(bf16[128,64]{0,1:T(8,128)(2,1)} %param.19) | copy-start | bytes 49156
  82.1 30.5 %all-to-all-start = ((bf16[2,512,256]{2,0,1:T(2,128)(2,1)}), bf16[2,512,256]{2,0,1:T(2,128)(2,1)S(1)}, u32[]{:S(2)}, u32[]{:S(2)}) async-start(bf16[2,512,256]{2,0,1:T(2,128)(2,1)} %all_gather.10), calls=%async_computation | async-start | bytes 1048576 | tf_op jit(solution)/shard_map/all_to_all | solution.py:62
  85.6 413.0 %reduce-scatter.2.cloned.1.call-start = ((), (), s32[]{:S(2)}) async-start(), calls=%async_computation.4 | async-start | bytes 12582912 | tf_op jit(solution)/shard_map/reduce_scatter | solution.py:104
  104.5 7.7 %copy-start.8 = (s32[128,4]{0,1:T(4,128)S(1)}, s32[128,4]{0,1:T(4,128)}, u32[]{:S(2)}) copy-start(s32[128,4]{0,1:T(4,128)} %param.14) | copy-start | bytes 6148
  279.5 17.4 %copy-start.2 = (f32[128,2,256,32]{2,3,1,0:T(8,128)S(1)}, f32[128,2,256,32]{2,3,1,0:T(8,128)}, u32[]{:S(2)}) copy-start(f32[128,2,256,32]{2,3,1,0:T(8,128)} %get-tuple-element.311) | copy-start | bytes 25165828 | tf_op jit(solution)/shard_map/while
  311.9 3.2 copy-start.3
  331.7 17.4 %copy-start.2 = (f32[128,2,256,32]{2,3,1,0:T(8,128)S(1)}, f32[128,2,256,32]{2,3,1,0:T(8,128)}, u32[]{:S(2)}) copy-start(f32[128,2,256,32]{2,3,1,0:T(8,128)} %get-tuple-element.311) | copy-start | bytes 25165828 | tf_op jit(solution)/shard_map/while
  364.1 3.2 copy-start.3
  383.8 17.4 %copy-start.2 = (f32[128,2,256,32]{2,3,1,0:T(8,128)S(1)}, f32[128,2,256,32]{2,3,1,0:T(8,128)}, u32[]{:S(2)}) copy-start(f32[128,2,256,32]{2,3,1,0:T(8,128)} %get-tuple-element.311) | copy-start | bytes 25165828 | tf_op jit(solution)/shard_map/while
  416.2 3.2 copy-start.3
  436.0 17.4 %copy-start.2 = (f32[128,2,256,32]{2,3,1,0:T(8,128)S(1)}, f32[128,2,256,32]{2,3,1,0:T(8,128)}, u32[]{:S(2)}) copy-start(f32[128,2,256,32]{2,3,1,0:T(8,128)} %get-tuple-element.311) | copy-start | bytes 25165828 | tf_op jit(solution)/shard_map/while
  468.4 3.2 copy-start.3
  471.8 5.8 %copy-start.4 = (f32[32768,64]{0,1:T(8,128)S(1)}, f32[32768,64]{0,1:T(8,128)}, u32[]{:S(2)}) copy-start(f32[32768,64]{0,1:T(8,128)} %fusion.22) | copy-start | bytes 25165828
Sparse Core Ops, SparseCore 0:
  45.2 112.2 all-gather.2
  159.1 103.9 all-gather.4
  482.3 16.2 reduce-scatter.1
where the time goes:
time: 506 us; the launch traced here: 505 us
  waiting for transfers between devices  166 us (33%)
  matrix products  164 us (32%)
  other arithmetic  102 us (20%)
  local copies, waits for them, and re-layouts  37.2 us (7%)
  blocking collectives  17.8 us (4%)
  between operations  14 us (3%)
    all_gather x1, waiting for transfers between devices, per_device(): piece_values = lax.all_gather(values_local, 'keys', axis=1, tiled=True)  106 us
    reduce_sum x4, other arithmetic, one_tile(): row_sum = row_sum * rescale + jnp.sum(weights, axis=-1)  67.2 us
    dot_general x4, matrix products, one_tile(): jnp.einsum('rjhd,rkhd->rhjk', queries, key_tile, preferred_element_type=j...  64.8 us
    dot_general x4, matrix products, one_tile(): jnp.einsum('rhjk,rkhd->rhjd', weights.astype(jnp.bfloat16), value_tile, p...  60.1 us
    all_gather x1, waiting for transfers between devices, per_device(): piece_keys = lax.all_gather(keys_local, 'keys', axis=1, tiled=True)  43.7 us
    all_gather x1, blocking collectives, per_device(): lax.all_gather(bias_local.astype(jnp.bfloat16), 'rows', axis=1, tiled=True)  17.8 us
    reduce_scatter x1, waiting for transfers between devices, per_device(): lax.psum_scatter(partial_out.astype(jnp.bfloat16), 'heads', scatter_dimen...  16.4 us
    unnamed x29, local copies, waits for them, and re-layouts  14 us
  transfers between devices with their start and end apart: 4, of which 3 were waited for; matrix products, arithmetic and copies ran while one was open for 9% of the time, Pallas kernels for 0%

commit v1 on v0

--- a/solution.py
+++ b/solution.py
@@ -67,8 +67,12 @@
         jnp.zeros((rows_dev, heads_dev, cols_dev), jnp.float32),
         jnp.zeros((rows_dev, heads_dev, cols_dev, HEAD_DIM), jnp.float32),
     )
-    piece_keys = lax.all_gather(keys_local, "keys", axis=1, tiled=True)
-    piece_values = lax.all_gather(values_local, "keys", axis=1, tiled=True)
+    take_windows = lambda payload, work_x: jnp.split(
+        jax.lax.all_gather(jnp.concatenate([payload, work_x], 0), "keys", axis=1, tiled=True),
+        [payload.shape[0]],
+        0,
+    )
+    piece_keys, piece_values = take_windows(keys_local, values_local)
 
     def one_tile(tile_index, state):
         row_max, row_sum, weighted = state

time: 506 us -> 524 us (1.036)
  local copies, waits for them, and re-layouts: 37.2 us -> 46.2 us
  other arithmetic: 102 us -> 110 us
    split x0 -> x1, local copies, waits for them, and re-layouts: none -> 11.8 us  [per_device(): jnp.split(jax.lax.all_gather(jnp.concatenate([payload, work_x], 0), 'keys...]
    concatenate x0 -> x1, other arithmetic: none -> 7.41 us  [per_device(): jnp.concatenate([payload, work_x], 0)]
    all_gather x2 -> x1, waiting for transfers between devices: 149 us -> 151 us  [per_device(): jax.lax.all_gather(jnp.concatenate([payload, work_x], 0), 'keys', axis=1,...]
  transfers between devices with their start and end apart: 4 -> 3, of which waited for: 3 -> 2; matrix products, arithmetic and copies ran while one was open for 9% -> 6% of each run, Pallas kernels for 0% -> 0%
where the time goes in v1:
time: 524 us; the launch traced here: 520 us
  waiting for transfers between devices  167 us (32%)
  matrix products  160 us (31%)
  other arithmetic  110 us (21%)
  local copies, waits for them, and re-layouts  46.2 us (9%)
  blocking collectives  18.1 us (3%)
  between operations  14.5 us (3%)
    all_gather x1, waiting for transfers between devices, per_device(): jax.lax.all_gather(jnp.concatenate([payload, work_x], 0), 'keys', axis=1,...  151 us
    reduce_sum x4, other arithmetic, one_tile(): row_sum = row_sum * rescale + jnp.sum(weights, axis=-1)  67.2 us
    dot_general x4, matrix products, one_tile(): jnp.einsum('rjhd,rkhd->rhjk', queries, key_tile, preferred_element_type=j...  64.8 us
    dot_general x4, matrix products, one_tile(): jnp.einsum('rhjk,rkhd->rhjd', weights.astype(jnp.bfloat16), value_tile, p...  60.1 us
    all_gather x1, blocking collectives, per_device(): lax.all_gather(bias_local.astype(jnp.bfloat16), 'rows', axis=1, tiled=True)  18.1 us
    reduce_scatter x1, waiting for transfers between devices, per_device(): lax.psum_scatter(partial_out.astype(jnp.bfloat16), 'heads', scatter_dimen...  16.4 us
    while x20, local copies, waits for them, and re-layouts  12.9 us
    split x1, local copies, waits for them, and re-layouts, per_device(): jnp.split(jax.lax.all_gather(jnp.concatenate([payload, work_x], 0), 'keys...  11.8 us
  transfers between devices with their start and end apart: 3, of which 2 were waited for; matrix products, arithmetic and copies ran while one was open for 6% of the time, Pallas kernels for 0%

profile of v1, /device:TPU:0, one launch (start us, length us, event | category | flops | bytes accessed | tf_op | source)
XLA Modules:
  0.0 520.0 jit_solution(9727672341363336073)
XLA Ops:
  6.5 5.8 %convert_reduce_fusion = f32[128,256]{1,0:T(8,128)S(1)} fusion(bf16[128,256,128]{2,1,0:T(8,128)(2,1)} %param.12), kind=kLoop, calls=%fused_computation.33 | loop fusion | flops 8355840 | bytes 8519680 | tf_op jit(solution)/shard_map/reduce_sum | solution.py:13
  12.4 0.0 slice-start.1
  12.4 10.9 %fusion.25 = f32[128,256]{1,0:T(8,128)S(1)} fusion(bf16[128,256,128]{2,1,0:T(8,128)(2,1)} %param.12, f32[128,256]{1,0:T(8,128)S(1)} %broadcast_multiply_fusion), kind=kLoop, calls=%fused_computation.36 | loop fusion | flops 16744448 | bytes 8650752 | tf_op jit(solution)/shard_map/reduce_sum | solution.py:14
  23.3 0.0 copy-start.5
  23.3 10.4 %fusion.27 = bf16[128,256,128]{2,1,0:T(8,128)(2,1)S(1)} fusion(bf16[128,256,128]{2,1,0:T(8,128)(2,1)S(1)} %bitcast.83, f32[128]{0:T(128)S(1)} %copy-done.9, f32[128,256]{1,0:T(8,128)S(1)} %add_rsqrt_fusion, f32[128,256]{1,0:T(8,128)S(1)} %broadcast_multiply_fusion), kind=kLoop, calls=%fused_computation.38 | loop fusion | flops 20971520 | bytes 17039872 | tf_op jit(solution)/shard_map/convert_element_type | solution.py:34
  33.8 3.0 convolution_convert_fusion.1
  36.8 1.1 copy.28
  37.9 4.4 copy.20
  42.3 3.0 convolution_convert_fusion
  45.3 1.1 copy.29
  46.4 4.4 copy.21
  50.8 7.4 %pad_maximum_fusion = bf16[256,256,2,32]{1,3,2,0:T(8,128)(2,1)} fusion(bf16[128,256,2,32]{1,3,2,0:T(8,128)(2,1)} %copy.21, bf16[128,256,2,32]{1,3,2,0:T(8,128)(2,1)} %copy.20), kind=kLoop, calls=%fused_computation.41 | loop fusion | flops 4194304 | bytes 16777216 | tf_op jit(solution)/shard_map/concatenate | solution.py:71
  58.2 0.0 all-gather.2.cloned.1.call-update
  58.3 0.6 copy-done.10
  58.9 5.8 %fusion.30 = bf16[2,128,256]{2,0,1:T(2,128)(2,1)S(1)} fusion(bf16[128,256,128]{2,1,0:T(8,128)(2,1)} %copy-done.1, bf16[128,2]{0,1:T(2,128)(2,1)S(1)} %copy-done.10), kind=kOutput, calls=%fused_computation.45 | convolution fusion | flops 16842752 | bytes 8520192 | tf_op jit(solution)/shard_map/rkc,ch->hrk/dot_general | solution.py:54
  64.7 18.1 %all_gather.7 = bf16[2,512,256]{2,0,1:T(2,128)(2,1)} all-gather(bf16[2,128,256]{2,0,1:T(2,128)(2,1)S(1)} %fusion.30), channel_id=1, replica_groups=mesh['groups'=2,'rows'=4,'keys'=2,'heads'=2] {'rows'}, dimensions={1}, use_global_device_ids=true | all-gather | bytes 655360 | tf_op jit(solution)/shard_map/all_gather | solution.py:55
  82.9 3.5 all-to-all-start
  86.4 0.0 reduce-scatter.2.cloned.1.call-start
  87.1 0.0 copy-done.7
  87.1 8.6 %fusion.21 = bf16[32768,64]{0,1:T(8,128)(2,1)} fusion(bf16[32768,128]{1,0:T(8,128)(2,1)} %bitcast.80, bf16[128,64]{0,1:T(8,128)(2,1)S(1)} %copy-done.7), kind=kOutput, calls=%fused_computation.28 | convolution fusion | flops 541065216 | bytes 12599296 | tf_op jit(solution)/shard_map/dot_general | solution.py:37
  95.7 0.0 copy-done.11
  95.7 9.8 %fusion.22 = f32[32768,64]{0,1:T(8,128)} fusion(bf16[32768,128]{1,0:T(8,128)(2,1)} %bitcast.81, bf16[128,64]{0,1:T(8,128)(2,1)S(1)} %copy-done.11), kind=kOutput, calls=%fused_computation.31 | convolution fusion | flops 543162368 | bytes 16793600 | tf_op jit(solution)/shard_map/dot_general | solution.py:51
  105.5 0.0 copy-start.8
  105.5 3.4 copy.30
  108.9 4.4 copy.23
  113.3 0.1 copy.19
  113.4 0.2 broadcast_in_dim.67
  113.6 0.1 fusion.31
  113.7 0.0 all-to-all-done
  113.7 0.4 convert_bitcast_fusion
  114.0 0.7 copy.22
  114.8 150.8 %all-gather.2.cloned.1.call-done = bf16[256,512,2,32]{1,3,2,0:T(8,128)(2,1)} async-done(((bf16[256,256,2,32]{1,3,2,0:T(8,128)(2,1)}), bf16[256,512,2,32]{1,3,2,0:T(8,128)(2,1)}) %all-gather.2.cloned.1.call-update) | async-done | bytes 16777232 | tf_op jit(solution)/shard_map/all_gather | solution.py:71
  265.6 11.8 %fusion.39 = (bf16[128,512,2,32]{1,3,2,0:T(8,128)(2,1)}, bf16[128,512,2,32]{1,3,2,0:T(8,128)(2,1)}) fusion(bf16[256,512,2,32]{1,3,2,0:T(8,128)(2,1)} %all-gather.2.cloned.1.call-done), kind=kLoop, calls=%fused_computation.62 | loop fusion | bytes 33554432 | tf_op jit(solution)/shard_map/split | solution.py:70
  277.4 208.6 %while.18 = (s32[]{:T(128)}, f32[128,2,256]{2,1,0:T(2,128)S(1)}, f32[128,2,256]{2,1,0:T(2,128)S(1)}, f32[128,2,256,32]{2,3,1,0:T(8,128)}, pred[128,512]{1,0:T(8,...) while((s32[]{:T(128)}, f32[128,2,256]{2,1,0:T(2,128)S(1)}, ...), condition=%wide.region_5.6_spmd.clone, body=%wide.region_2.5_spmd.clone.sunk | while | flops 1189412864 | bytes 198525168 | solution.py:101
  277.4 16.2 %fusion.61 = (f32[128,2,256]{2,1,0:T(2,128)S(1)}, f32[128,2,128,256]{3,2,1,0:T(8,128)}) fusion(f32[2,256,128]{1,2,0:T(8,128)S(1)} %constant_dynamic-slice_fusion.4, pred[128,128]{1,0:T(8,128)(4,1)S(1)} %constant_dynamic-slice_fusion.5, bf16[128,256,2,32]{1,3,2,0:T(8,128)(2,1)} %get-tuple-element.329, ...), kind=kOutput, calls=%fused_computation.3.clone.1 | convolution fusion | flops 561971200 | bytes 40386564 | tf_op jit(solution)/shard_map/while/body/eval_jaxpr/rjhd,rkhd->rhjk/dot_general | solution.py:85
  293.7 0.2 fusion.62
  293.9 16.8 %fusion.63 = f32[128,2,256]{2,1,0:T(2,128)S(1)} fusion(f32[128,2,128,256]{3,2,1,0:T(8,128)} %get-tuple-element.294, f32[128,2,256]{2,1,0:T(2,128)S(1)} %fusion.62, f32[2,256,128]{1,2,0:T(8,128)S(1)} %constant_dynamic-slice_fusion.4, pred[128,128]{1,0:T(8,128)(4,1)S(1)} %constant_dynamic-slice_fusion.5), kind=kLoop, calls=%fused_computation.5.clone.1 | loop fusion | flops 41877504 | bytes 34357248 | tf_op jit(solution)/shard_map/while/body/eval_jaxpr/reduce_sum | solution.py:92
  310.7 0.6 fusion.64
  311.2 15.0 %fusion.65 = f32[128,2,256,32]{2,3,1,0:T(8,128)S(1)} fusion(f32[128,2,256,32]{2,3,1,0:T(8,128)S(1)} %copy-done.2, f32[128,2,256]{2,1,0:T(2,128)S(1)} %get-tuple-element.296, pred[]{:T(512)S(6)} %compare.4, f32[128,2,128,256]{3,2,1,0:T(8,128)} %get-tuple-element.294, f32[128,2,256]{2,1,0:T(2,128)S(1)} %fusion.62, ...), kind=kOutput, calls=%fused_computation.9.clone.1 | convolution fusion | flops 585105408 | bytes 53231620 | tf_op jit(solution)/shard_map/while/body/eval_jaxpr/rhjk,rkhd->rhjd/dot_general | solution.py:93
  326.3 3.2 copy-done.3
  329.6 16.2 %fusion.61 = (f32[128,2,256]{2,1,0:T(2,128)S(1)}, f32[128,2,128,256]{3,2,1,0:T(8,128)}) fusion(f32[2,256,128]{1,2,0:T(8,128)S(1)} %constant_dynamic-slice_fusion.4, pred[128,128]{1,0:T(8,128)(4,1)S(1)} %constant_dynamic-slice_fusion.5, bf16[128,256,2,32]{1,3,2,0:T(8,128)(2,1)} %get-tuple-element.329, ...), kind=kOutput, calls=%fused_computation.3.clone.1 | convolution fusion | flops 561971200 | bytes 40386564 | tf_op jit(solution)/shard_map/while/body/eval_jaxpr/rjhd,rkhd->rhjk/dot_general | solution.py:85
  345.8 0.2 fusion.62
  346.0 16.8 %fusion.63 = f32[128,2,256]{2,1,0:T(2,128)S(1)} fusion(f32[128,2,128,256]{3,2,1,0:T(8,128)} %get-tuple-element.294, f32[128,2,256]{2,1,0:T(2,128)S(1)} %fusion.62, f32[2,256,128]{1,2,0:T(8,128)S(1)} %constant_dynamic-slice_fusion.4, pred[128,128]{1,0:T(8,128)(4,1)S(1)} %constant_dynamic-slice_fusion.5), kind=kLoop, calls=%fused_computation.5.clone.1 | loop fusion | flops 41877504 | bytes 34357248 | tf_op jit(solution)/shard_map/while/body/eval_jaxpr/reduce_sum | solution.py:92
  362.8 0.6 fusion.64
  363.4 15.0 %fusion.65 = f32[128,2,256,32]{2,3,1,0:T(8,128)S(1)} fusion(f32[128,2,256,32]{2,3,1,0:T(8,128)S(1)} %copy-done.2, f32[128,2,256]{2,1,0:T(2,128)S(1)} %get-tuple-element.296, pred[]{:T(512)S(6)} %compare.4, f32[128,2,128,256]{3,2,1,0:T(8,128)} %get-tuple-element.294, f32[128,2,256]{2,1,0:T(2,128)S(1)} %fusion.62, ...), kind=kOutput, calls=%fused_computation.9.clone.1 | convolution fusion | flops 585105408 | bytes 53231620 | tf_op jit(solution)/shard_map/while/body/eval_jaxpr/rhjk,rkhd->rhjd/dot_general | solution.py:93
  378.5 3.2 copy-done.3
  381.8 16.2 %fusion.61 = (f32[128,2,256]{2,1,0:T(2,128)S(1)}, f32[128,2,128,256]{3,2,1,0:T(8,128)}) fusion(f32[2,256,128]{1,2,0:T(8,128)S(1)} %constant_dynamic-slice_fusion.4, pred[128,128]{1,0:T(8,128)(4,1)S(1)} %constant_dynamic-slice_fusion.5, bf16[128,256,2,32]{1,3,2,0:T(8,128)(2,1)} %get-tuple-element.329, ...), kind=kOutput, calls=%fused_computation.3.clone.1 | convolution fusion | flops 561971200 | bytes 40386564 | tf_op jit(solution)/shard_map/while/body/eval_jaxpr/rjhd,rkhd->rhjk/dot_general | solution.py:85
  398.0 0.2 fusion.62
  398.2 16.8 %fusion.63 = f32[128,2,256]{2,1,0:T(2,128)S(1)} fusion(f32[128,2,128,256]{3,2,1,0:T(8,128)} %get-tuple-element.294, f32[128,2,256]{2,1,0:T(2,128)S(1)} %fusion.62, f32[2,256,128]{1,2,0:T(8,128)S(1)} %constant_dynamic-slice_fusion.4, pred[128,128]{1,0:T(8,128)(4,1)S(1)} %constant_dynamic-slice_fusion.5), kind=kLoop, calls=%fused_computation.5.clone.1 | loop fusion | flops 41877504 | bytes 34357248 | tf_op jit(solution)/shard_map/while/body/eval_jaxpr/reduce_sum | solution.py:92
  415.0 0.6 fusion.64
  415.6 15.0 %fusion.65 = f32[128,2,256,32]{2,3,1,0:T(8,128)S(1)} fusion(f32[128,2,256,32]{2,3,1,0:T(8,128)S(1)} %copy-done.2, f32[128,2,256]{2,1,0:T(2,128)S(1)} %get-tuple-element.296, pred[]{:T(512)S(6)} %compare.4, f32[128,2,128,256]{3,2,1,0:T(8,128)} %get-tuple-element.294, f32[128,2,256]{2,1,0:T(2,128)S(1)} %fusion.62, ...), kind=kOutput, calls=%fused_computation.9.clone.1 | convolution fusion | flops 585105408 | bytes 53231620 | tf_op jit(solution)/shard_map/while/body/eval_jaxpr/rhjk,rkhd->rhjd/dot_general | solution.py:93
  430.6 3.2 copy-done.3
  433.9 16.2 %fusion.61 = (f32[128,2,256]{2,1,0:T(2,128)S(1)}, f32[128,2,128,256]{3,2,1,0:T(8,128)}) fusion(f32[2,256,128]{1,2,0:T(8,128)S(1)} %constant_dynamic-slice_fusion.4, pred[128,128]{1,0:T(8,128)(4,1)S(1)} %constant_dynamic-slice_fusion.5, bf16[128,256,2,32]{1,3,2,0:T(8,128)(2,1)} %get-tuple-element.329, ...), kind=kOutput, calls=%fused_computation.3.clone.1 | convolution fusion | flops 561971200 | bytes 40386564 | tf_op jit(solution)/shard_map/while/body/eval_jaxpr/rjhd,rkhd->rhjk/dot_general | solution.py:85
  450.1 0.2 fusion.62
  450.3 16.8 %fusion.63 = f32[128,2,256]{2,1,0:T(2,128)S(1)} fusion(f32[128,2,128,256]{3,2,1,0:T(8,128)} %get-tuple-element.294, f32[128,2,256]{2,1,0:T(2,128)S(1)} %fusion.62, f32[2,256,128]{1,2,0:T(8,128)S(1)} %constant_dynamic-slice_fusion.4, pred[128,128]{1,0:T(8,128)(4,1)S(1)} %constant_dynamic-slice_fusion.5), kind=kLoop, calls=%fused_computation.5.clone.1 | loop fusion | flops 41877504 | bytes 34357248 | tf_op jit(solution)/shard_map/while/body/eval_jaxpr/reduce_sum | solution.py:92
  467.1 0.6 fusion.64
  467.7 15.0 %fusion.65 = f32[128,2,256,32]{2,3,1,0:T(8,128)S(1)} fusion(f32[128,2,256,32]{2,3,1,0:T(8,128)S(1)} %copy-done.2, f32[128,2,256]{2,1,0:T(2,128)S(1)} %get-tuple-element.296, pred[]{:T(512)S(6)} %compare.4, f32[128,2,128,256]{3,2,1,0:T(8,128)} %get-tuple-element.294, f32[128,2,256]{2,1,0:T(2,128)S(1)} %fusion.62, ...), kind=kOutput, calls=%fused_computation.9.clone.1 | convolution fusion | flops 585105408 | bytes 53231620 | tf_op jit(solution)/shard_map/while/body/eval_jaxpr/rhjk,rkhd->rhjd/dot_general | solution.py:93
  482.8 3.2 copy-done.3
  486.0 0.1 broadcast_maximum_fusion
  486.1 5.0 divide_convert_fusion
  491.2 0.7 copy-done.4
  491.9 4.6 convolution_convert_fusion.2
  496.5 0.0 reduce-scatter.2.cloned.1.call-update
  496.5 16.4 %reduce-scatter.2.cloned.1.call-done = bf16[128,128,128]{2,1,0:T(8,128)(2,1)} async-done(((bf16[128,256,128]{2,1,0:T(8,128)(2,1)}), bf16[128,128,128]{2,1,0:T(8,128)(2,1)}) %reduce-scatter.2.cloned.1.call-update) | async-done | bytes 4194320 | tf_op jit(solution)/shard_map/reduce_scatter | solution.py:108
  (50 shorter events, 0.3 us)
Async XLA Ops:
  6.5 484.6 %copy-start = (bf16[128,128]{1,0:T(8,128)(2,1)S(1)}, bf16[128,128]{1,0:T(8,128)(2,1)}, u32[]{:S(2)}) copy-start(bf16[128,128]{1,0:T(8,128)(2,1)} %param.21) | copy-start | bytes 98308
  6.5 16.8 %copy-start.9 = (f32[128]{0:T(128)S(1)}, f32[128]{0:T(128)}, u32[]{:S(2)}) copy-start(f32[128]{0:T(128)} %param.15) | copy-start | bytes 1540
  6.5 259.0 %all-gather.2.cloned.1.call-start = ((), (), s32[]{:S(2)}) async-start(), calls=%async_computation.2 | async-start | bytes 25165824 | tf_op jit(solution)/shard_map/all_gather | solution.py:71
  6.5 16.8 %slice-start = ((s8[8388608]{0:T(1024)(128)(4,1)}), s8[4194304]{0:T(1024)(128)(4,1)S(1)}, s32[]{:S(2)}) async-start(s8[8388608]{0:T(1024)(128)(4,1)} %bitcast.82), calls=%async_computation.4 | async-start | bytes 8388608
  12.4 10.9 %slice-start.1 = ((s8[8388608]{0:T(1024)(128)(4,1)}), s8[4194304]{0:T(1024)(128)(4,1)S(1)}, s32[]{:S(2)}) async-start(s8[8388608]{0:T(1024)(128)(4,1)} %bitcast.82), calls=%async_computation.5 | async-start | bytes 8388608
  23.3 10.4 %copy-start.5 = (bf16[128,64]{0,1:T(8,128)(2,1)S(1)}, bf16[128,64]{0,1:T(8,128)(2,1)}, u32[]{:S(2)}) copy-start(bf16[128,64]{0,1:T(8,128)(2,1)} %param.17) | copy-start | bytes 49156
  33.7 8.5 %copy-start.1 = (bf16[128,256,128]{2,1,0:T(8,128)(2,1)}, bf16[128,256,128]{2,1,0:T(8,128)(2,1)S(1)}, u32[]{:S(2)}) copy-start(bf16[128,256,128]{2,1,0:T(8,128)(2,1)S(1)} %fusion.27) | copy-start | bytes 25165828
  36.8 5.5 %copy-start.6 = (bf16[128,64]{0,1:T(8,128)(2,1)S(1)}, bf16[128,64]{0,1:T(8,128)(2,1)}, u32[]{:S(2)}) copy-start(bf16[128,64]{0,1:T(8,128)(2,1)} %param.18) | copy-start | bytes 49156
  58.2 0.7 copy-start.10
  58.9 28.2 %copy-start.7 = (bf16[128,64]{0,1:T(8,128)(2,1)S(1)}, bf16[128,64]{0,1:T(8,128)(2,1)}, u32[]{:S(2)}) copy-start(bf16[128,64]{0,1:T(8,128)(2,1)} %param.16) | copy-start | bytes 49156
  64.7 30.9 %copy-start.11 = (bf16[128,64]{0,1:T(8,128)(2,1)S(1)}, bf16[128,64]{0,1:T(8,128)(2,1)}, u32[]{:S(2)}) copy-start(bf16[128,64]{0,1:T(8,128)(2,1)} %param.19) | copy-start | bytes 49156
  82.9 30.8 %all-to-all-start = ((bf16[2,512,256]{2,0,1:T(2,128)(2,1)}), bf16[2,512,256]{2,0,1:T(2,128)(2,1)S(1)}, u32[]{:S(2)}, u32[]{:S(2)}) async-start(bf16[2,512,256]{2,0,1:T(2,128)(2,1)} %all_gather.7), calls=%async_computation | async-start | bytes 1048576 | tf_op jit(solution)/shard_map/all_to_all | solution.py:62
  86.4 426.6 %reduce-scatter.2.cloned.1.call-start = ((), (), s32[]{:S(2)}) async-start(), calls=%async_computation.3 | async-start | bytes 12582912 | tf_op jit(solution)/shard_map/reduce_scatter | solution.py:108
  105.5 7.8 %copy-start.8 = (s32[128,4]{0,1:T(4,128)S(1)}, s32[128,4]{0,1:T(4,128)}, u32[]{:S(2)}) copy-start(s32[128,4]{0,1:T(4,128)} %param.14) | copy-start | bytes 6148
  293.9 17.4 %copy-start.2 = (f32[128,2,256,32]{2,3,1,0:T(8,128)S(1)}, f32[128,2,256,32]{2,3,1,0:T(8,128)}, u32[]{:S(2)}) copy-start(f32[128,2,256,32]{2,3,1,0:T(8,128)} %get-tuple-element.313) | copy-start | bytes 25165828 | tf_op jit(solution)/shard_map/while
  326.3 3.2 copy-start.3
  346.0 17.4 %copy-start.2 = (f32[128,2,256,32]{2,3,1,0:T(8,128)S(1)}, f32[128,2,256,32]{2,3,1,0:T(8,128)}, u32[]{:S(2)}) copy-start(f32[128,2,256,32]{2,3,1,0:T(8,128)} %get-tuple-element.313) | copy-start | bytes 25165828 | tf_op jit(solution)/shard_map/while
  378.4 3.2 copy-start.3
  398.2 17.4 %copy-start.2 = (f32[128,2,256,32]{2,3,1,0:T(8,128)S(1)}, f32[128,2,256,32]{2,3,1,0:T(8,128)}, u32[]{:S(2)}) copy-start(f32[128,2,256,32]{2,3,1,0:T(8,128)} %get-tuple-element.313) | copy-start | bytes 25165828 | tf_op jit(solution)/shard_map/while
  430.6 3.2 copy-start.3
  450.3 17.4 %copy-start.2 = (f32[128,2,256,32]{2,3,1,0:T(8,128)S(1)}, f32[128,2,256,32]{2,3,1,0:T(8,128)}, u32[]{:S(2)}) copy-start(f32[128,2,256,32]{2,3,1,0:T(8,128)} %get-tuple-element.313) | copy-start | bytes 25165828 | tf_op jit(solution)/shard_map/while
  482.8 3.2 copy-start.3
  486.1 5.8 %copy-start.4 = (f32[32768,64]{0,1:T(8,128)S(1)}, f32[32768,64]{0,1:T(8,128)}, u32[]{:S(2)}) copy-start(f32[32768,64]{0,1:T(8,128)} %fusion.22) | copy-start | bytes 25165828
Sparse Core Ops, SparseCore 0:
  58.4 207.1 all-gather.1
  496.7 16.2 reduce-scatter.1
